TPU v7x, 128 devices: a whole 4x4x4 slice. The times are simulated.
128 devices in a mesh: row: 16 (over x, y), col: 8 (over z, core).
Axes of the slice: x: 4, y: 4, z: 4, core: 2. Of those that a mesh axis runs over, the one named last changes fastest.
Arguments:
- tokens: bfloat16 [32, 8192], P(None, 'row'), may hold values from -6 to 6
- gain: float32 [8192], P('row'), may hold values from 0.24 to 4.5
- gate_weight: bfloat16 [8192, 28672], P('row', 'col'), may hold values from -0.0625 to 0.0625
- up_weight: bfloat16 [8192, 28672], P('row', 'col'), may hold values from -0.0625 to 0.0625
- down_weight: bfloat16 [28672, 8192], P('col', 'row'), may hold values from -0.03125 to 0.03125
- probes: float32 [4, 32, 8192], P(None, None, 'row'), may hold values from -6 to 6
Outputs:
- basis: float32 [4, 32, 8192], P(None, None, 'row')
- stretch: float32 [4], replicated
All inputs are finite; a program needn't handle non-finite values.
Results may differ from a plain program's by a relative error of at most 0.0085.
Values may be sent and summed in bfloat16 or wider, within the bound.
A program may use at most 64 MiB of HBM per device.

v0:
```python
import functools

import jax
import jax.numpy as jnp
from jax import lax
from jax.sharding import Mesh
from jax.sharding import PartitionSpec as P

ITERS = 3
ROW = ("row_0", "row_1")


epsilon = 1e-06


def in_blocks(array, dim, count):
    dims = array.shape
    parts = array.reshape(*dims[:dim], count, dims[dim] // count, *dims[dim + 1 :])
    return jnp.moveaxis(parts, dim, 0)


def summed_on_arrival(array, axis, dim):
    count = lax.axis_size(axis)
    parts = lax.all_to_all(in_blocks(array, dim, count), axis, 0, 0, tiled=True)
    return jnp.sum(parts, axis=0)


def from_everyone(array, axis):
    copies = jnp.broadcast_to(array, (lax.axis_size(axis), *array.shape))
    return lax.all_to_all(copies, axis, split_axis=0, concat_axis=0, tiled=True)


def joined_along(parts, dim):
    dims = list(parts.shape[1:])
    dims[dim] *= parts.shape[0]
    return jnp.moveaxis(parts, 0, dim).reshape(dims)


def gather_directly(array, axis, dim):
    parts = from_everyone(array, axis)
    return joined_along(parts, dim)


def of_everyone(array, axis):
    return from_everyone(array, axis).sum(axis=0)


def by_axis(array, axes):
    return functools.reduce(lax.psum, axes, array)


def local(tokens, gain, gate_weight, up_weight, down_weight, probes):
    scaled = (tokens.astype(jnp.float32) * gain).astype(jnp.bfloat16)
    gate_part = jnp.dot(scaled, gate_weight, preferred_element_type=jnp.float32)
    up_part = jnp.dot(scaled, up_weight, preferred_element_type=jnp.float32)
    gate, up = lax.psum((gate_part, up_part), ROW)
    sigmoid_gate = 1.0 / (1.0 + jnp.exp(-gate))
    activated = gate * sigmoid_gate
    slope = sigmoid_gate * (1.0 + gate * (1.0 - sigmoid_gate)) * up
    probe_count, token_count, local_width = probes.shape
    row_count = probe_count * token_count
    slope_all = jnp.tile(slope, (probe_count, 1))
    activated_all = jnp.tile(activated, (probe_count, 1))
    entries = token_count * local_width * lax.axis_size(ROW)
    transposed = (((1,), (1,)), ((), ()))
    current = probes
    level = jnp.zeros((probe_count,), jnp.float32)
    for sweep in range(ITERS):
        pushed = (current * gain).astype(jnp.bfloat16).reshape(row_count, local_width)
        gate_tan = jnp.dot(pushed, gate_weight, preferred_element_type=jnp.float32)
        up_tan = jnp.dot(pushed, up_weight, preferred_element_type=jnp.float32)
        joined = slope_all * gate_tan + activated_all * up_tan
        hidden = summed_on_arrival(joined, ROW, 0).astype(jnp.bfloat16)
        tangent_part = jnp.dot(
            gather_directly(hidden, ROW, 0), down_weight, preferred_element_type=jnp.float32
        )
        tangent = of_everyone(tangent_part, "col").astype(jnp.bfloat16)
        back_part = lax.dot_general(
            tangent, down_weight, transposed, preferred_element_type=jnp.float32
        )
        back_share = summed_on_arrival(back_part, ROW, 0).astype(jnp.bfloat16)
        piece = gather_directly(back_share, ROW, 0)
        gate_pull = (slope_all * piece).astype(jnp.bfloat16)
        up_pull = (activated_all * piece).astype(jnp.bfloat16)
        result = lax.dot_general(
            gate_pull, gate_weight, transposed, preferred_element_type=jnp.float32
        )
        pulled_part = result + lax.dot_general(
            up_pull, up_weight, transposed, preferred_element_type=jnp.float32
        )
        pulled = of_everyone(pulled_part, "col")
        grown = pulled.reshape(probe_count, token_count, local_width) * gain
        squares = jnp.sum(grown * grown, axis=(1, 2))
        level = by_axis(squares, ROW) / entries
        current = grown * lax.rsqrt(level + epsilon)[:, None, None]
    return (current, jnp.sqrt(level))


def solution(mesh):
    torus = Mesh(mesh.devices.reshape(4, 4, mesh.shape["col"]), ("row_0", "row_1", "col"))
    in_specs = (
        P(None, ROW),
        P(ROW),
        P(ROW, "col"),
        P(ROW, "col"),
        P("col", ROW),
        P(None, None, ROW),
    )
    out_specs = (P(None, None, ROW), P())
    return jax.shard_map(local, mesh=torus, in_specs=in_specs, out_specs=out_specs, check_vma=False)
```

profile of v0, /device:TPU:1, one launch (start us, length us, event | category | flops | bytes accessed | tf_op | source)
XLA Modules:
  0.0 651.4 jit_solution(17898869282795394094)
XLA Ops:
  12.6 88.0 %all-reduce.3.cloned.1.call-done = (f32[32,3584]{1,0:T(8,128)}, f32[32,3584]{1,0:T(8,128)}) async-done(((f32[32,3584]{1,0:T(8,128)}, f32[32,3584]{1,0:T(8,128)}), (f32[32,3584]{1,0:T(8,128)}, f32[32,3584]{1,0:T(8,128)})) %all-reduce.3.cloned.1.call-update) | async-done | bytes 917520 | tf_op jit(solution)/shard_map/psum | solution.py:56
  105.8 25.9 %all_to_all.90 = f32[16,8,3584]{2,1,0:T(8,128)S(1)} all-to-all(f32[16,8,3584]{2,1,0:T(8,128)S(1)} %fusion.3), channel_id=1, replica_groups=mesh['row_0'=4,'row_1'=4,'col'=8] {'row_0','row_1'}, dimensions={0} | all-to-all | bytes 3670016 | tf_op jit(solution)/shard_map/all_to_all | solution.py:24
  131.8 14.4 %all_to_all.91 = bf16[16,8,3584]{2,1,0:T(8,128)(2,1)S(1)} all-to-all(bf16[16,8,3584]{2,1,0:T(8,128)(2,1)S(1)} %broadcast_in_dim.46), channel_id=1, replica_groups=mesh['row_0'=4,'row_1'=4,'col'=8] {'row_0','row_1'}, dimensions={0} | all-to-all | bytes 1835008 | tf_op jit(solution)/shard_map/all_to_all | solution.py:30
  149.2 36.0 %all_to_all.92 = f32[8,128,512]{2,1,0:T(8,128)S(1)} all-to-all(f32[8,128,512]{2,1,0:T(8,128)S(1)} %broadcast_in_dim.47), channel_id=1, replica_groups=mesh['row_0'=4,'row_1'=4,'col'=8] {'col'}, dimensions={0} | all-to-all | bytes 4194304 | tf_op jit(solution)/shard_map/all_to_all | solution.py:30
  188.8 26.8 %all_to_all.93 = f32[16,8,3584]{2,1,0:T(8,128)S(1)} all-to-all(f32[16,8,3584]{2,1,0:T(8,128)S(1)} %convolution_bitcast_fusion.2), channel_id=1, replica_groups=mesh['row_0'=4,'row_1'=4,'col'=8] {'row_0','row_1'}, dimensions={0} | all-to-all | bytes 3670016 | tf_op jit(solution)/shard_map/all_to_all | solution.py:24
  215.7 16.0 %all_to_all.94 = bf16[16,8,3584]{2,1,0:T(8,128)(2,1)S(1)} all-to-all(bf16[16,8,3584]{2,1,0:T(8,128)(2,1)S(1)} %broadcast_in_dim.48), channel_id=1, replica_groups=mesh['row_0'=4,'row_1'=4,'col'=8] {'row_0','row_1'}, dimensions={0} | all-to-all | bytes 1835008 | tf_op jit(solution)/shard_map/all_to_all | solution.py:30
  237.4 33.1 %all_to_all.95 = f32[8,128,512]{2,1,0:T(8,128)S(1)} all-to-all(f32[8,128,512]{2,1,0:T(8,128)S(1)} %broadcast_in_dim.49), channel_id=1, replica_groups=mesh['row_0'=4,'row_1'=4,'col'=8] {'col'}, dimensions={0} | all-to-all | bytes 4194304 | tf_op jit(solution)/shard_map/all_to_all | solution.py:30
  271.0 7.0 %psum.58 = f32[4]{0:T(128)S(1)} all-reduce(f32[4]{0:T(128)S(1)} %reduce_sum.162), channel_id=1, replica_groups=mesh['row_0'=4,'row_1'=4,'col'=8] {'row_0'}, use_global_device_ids=true, to_apply=%region_8.0 | all-reduce | flops 4 | bytes 32 | tf_op jit(solution)/shard_map/psum | solution.py:49
  278.1 6.4 psum.59
  288.6 22.8 %all_to_all.96 = f32[16,8,3584]{2,1,0:T(8,128)S(1)} all-to-all(f32[16,8,3584]{2,1,0:T(8,128)S(1)} %fusion.4), channel_id=1, replica_groups=mesh['row_0'=4,'row_1'=4,'col'=8] {'row_0','row_1'}, dimensions={0} | all-to-all | bytes 3670016 | tf_op jit(solution)/shard_map/all_to_all | solution.py:24
  311.5 14.1 %all_to_all.97 = bf16[16,8,3584]{2,1,0:T(8,128)(2,1)S(1)} all-to-all(bf16[16,8,3584]{2,1,0:T(8,128)(2,1)S(1)} %broadcast_in_dim.50), channel_id=1, replica_groups=mesh['row_0'=4,'row_1'=4,'col'=8] {'row_0','row_1'}, dimensions={0} | all-to-all | bytes 1835008 | tf_op jit(solution)/shard_map/all_to_all | solution.py:30
  328.6 36.1 %all_to_all.98 = f32[8,128,512]{2,1,0:T(8,128)S(1)} all-to-all(f32[8,128,512]{2,1,0:T(8,128)S(1)} %broadcast_in_dim.51), channel_id=1, replica_groups=mesh['row_0'=4,'row_1'=4,'col'=8] {'col'}, dimensions={0} | all-to-all | bytes 4194304 | tf_op jit(solution)/shard_map/all_to_all | solution.py:30
  368.2 26.9 %all_to_all.99 = f32[16,8,3584]{2,1,0:T(8,128)S(1)} all-to-all(f32[16,8,3584]{2,1,0:T(8,128)S(1)} %convolution_bitcast_fusion.1), channel_id=1, replica_groups=mesh['row_0'=4,'row_1'=4,'col'=8] {'row_0','row_1'}, dimensions={0} | all-to-all | bytes 3670016 | tf_op jit(solution)/shard_map/all_to_all | solution.py:24
  395.2 16.6 %all_to_all.100 = bf16[16,8,3584]{2,1,0:T(8,128)(2,1)S(1)} all-to-all(bf16[16,8,3584]{2,1,0:T(8,128)(2,1)S(1)} %broadcast_in_dim.52), channel_id=1, replica_groups=mesh['row_0'=4,'row_1'=4,'col'=8] {'row_0','row_1'}, dimensions={0} | all-to-all | bytes 1835008 | tf_op jit(solution)/shard_map/all_to_all | solution.py:30
  417.5 32.4 %all_to_all.101 = f32[8,128,512]{2,1,0:T(8,128)S(1)} all-to-all(f32[8,128,512]{2,1,0:T(8,128)S(1)} %broadcast_in_dim.53), channel_id=1, replica_groups=mesh['row_0'=4,'row_1'=4,'col'=8] {'col'}, dimensions={0} | all-to-all | bytes 4194304 | tf_op jit(solution)/shard_map/all_to_all | solution.py:30
  450.4 7.0 %psum.60 = f32[4]{0:T(128)S(1)} all-reduce(f32[4]{0:T(128)S(1)} %reduce_sum.169), channel_id=1, replica_groups=mesh['row_0'=4,'row_1'=4,'col'=8] {'row_0'}, use_global_device_ids=true, to_apply=%region_16.0 | all-reduce | flops 4 | bytes 32 | tf_op jit(solution)/shard_map/psum | solution.py:49
  457.4 6.4 psum.61
  467.9 22.9 %all_to_all.102 = f32[16,8,3584]{2,1,0:T(8,128)S(1)} all-to-all(f32[16,8,3584]{2,1,0:T(8,128)S(1)} %fusion.5), channel_id=1, replica_groups=mesh['row_0'=4,'row_1'=4,'col'=8] {'row_0','row_1'}, dimensions={0} | all-to-all | bytes 3670016 | tf_op jit(solution)/shard_map/all_to_all | solution.py:24
  491.0 14.1 %all_to_all.103 = bf16[16,8,3584]{2,1,0:T(8,128)(2,1)S(1)} all-to-all(bf16[16,8,3584]{2,1,0:T(8,128)(2,1)S(1)} %broadcast_in_dim.54), channel_id=1, replica_groups=mesh['row_0'=4,'row_1'=4,'col'=8] {'row_0','row_1'}, dimensions={0} | all-to-all | bytes 1835008 | tf_op jit(solution)/shard_map/all_to_all | solution.py:30
  508.0 36.0 %all_to_all.104 = f32[8,128,512]{2,1,0:T(8,128)S(1)} all-to-all(f32[8,128,512]{2,1,0:T(8,128)S(1)} %broadcast_in_dim.55), channel_id=1, replica_groups=mesh['row_0'=4,'row_1'=4,'col'=8] {'col'}, dimensions={0} | all-to-all | bytes 4194304 | tf_op jit(solution)/shard_map/all_to_all | solution.py:30
  547.6 26.8 %all_to_all.105 = f32[16,8,3584]{2,1,0:T(8,128)S(1)} all-to-all(f32[16,8,3584]{2,1,0:T(8,128)S(1)} %convolution_bitcast_fusion), channel_id=1, replica_groups=mesh['row_0'=4,'row_1'=4,'col'=8] {'row_0','row_1'}, dimensions={0} | all-to-all | bytes 3670016 | tf_op jit(solution)/shard_map/all_to_all | solution.py:24
  574.6 16.6 %all_to_all.106 = bf16[16,8,3584]{2,1,0:T(8,128)(2,1)S(1)} all-to-all(bf16[16,8,3584]{2,1,0:T(8,128)(2,1)S(1)} %broadcast_in_dim.56), channel_id=1, replica_groups=mesh['row_0'=4,'row_1'=4,'col'=8] {'row_0','row_1'}, dimensions={0} | all-to-all | bytes 1835008 | tf_op jit(solution)/shard_map/all_to_all | solution.py:30
  596.8 32.4 %all_to_all.107 = f32[8,128,512]{2,1,0:T(8,128)S(1)} all-to-all(f32[8,128,512]{2,1,0:T(8,128)S(1)} %broadcast_in_dim.57), channel_id=1, replica_groups=mesh['row_0'=4,'row_1'=4,'col'=8] {'col'}, dimensions={0} | all-to-all | bytes 4194304 | tf_op jit(solution)/shard_map/all_to_all | solution.py:30
  629.8 7.0 %psum.62 = f32[4]{0:T(128)S(1)} all-reduce(f32[4]{0:T(128)S(1)} %reduce_sum.176), channel_id=1, replica_groups=mesh['row_0'=4,'row_1'=4,'col'=8] {'row_0'}, use_global_device_ids=true, to_apply=%region_24.25 | all-reduce | flops 4 | bytes 32 | tf_op jit(solution)/shard_map/psum | solution.py:49
  (95 shorter events, 65.1 us)
Async XLA Ops:
  7.2 3.8 copy-start.11
  7.2 3.8 copy-start.12
  7.2 93.4 %all-reduce.3.cloned.1.call-start = ((), (), s32[]{:S(2)}) async-start(), calls=%async_computation.18 | async-start | bytes 1835008 | tf_op jit(solution)/shard_map/psum | solution.py:56
  7.2 3.8 copy-start.6
  11.0 1.6 copy-start.10
  101.9 3.1 copy-start
  231.8 2.0 copy-start.7
  233.8 2.0 copy-start.1
  284.7 3.1 copy-start.2
  411.8 2.0 copy-start.8
  413.9 2.0 copy-start.3
  464.0 3.1 copy-start.4
  591.2 2.0 copy-start.9
  593.2 2.0 copy-start.5
Sparse Core Ops, SparseCore 0:
  12.7 87.8 all-reduce.2
where the time goes:
time: 656 us; the launch traced here: 651 us
  blocking collectives  490 us (75%)
  waiting for transfers between devices  88 us (13%)
  matrix products  41.8 us (6%)
  between operations  14.4 us (2%)
  local copies, waits for them, and re-layouts  10.8 us (2%)
    all_to_all x12, blocking collectives, from_everyone(): return lax.all_to_all(copies, axis, split_axis=0, concat_axis=0, tiled=True)  298 us
    all_to_all x6, blocking collectives, summed_on_arrival(): parts = lax.all_to_all(in_blocks(array, dim, count), axis, 0, 0, tiled=True)  152 us
    psum x1, waiting for transfers between devices, local(): gate, up = lax.psum((gate_part, up_part), ROW)  88 us
    psum x6, blocking collectives, by_axis(): return functools.reduce(lax.psum, axes, array)  40.3 us
  transfers between devices with their start and end apart: 1, of which 1 were waited for; matrix products, arithmetic and copies ran while one was open for 0% of the time, Pallas kernels for 0%

commit v1 on v0

v1 whole, which is shorter than its diff:
```python
import functools

import jax
import jax.numpy as jnp
from jax import lax
from jax.experimental import pallas as pl
from jax.experimental.pallas import tpu as pltpu
from jax.sharding import Mesh
from jax.sharding import PartitionSpec as P

ITERS = 3
EPSILON = 1e-06
MESH = pl.DeviceIdType.MESH
F32 = jnp.float32
BF16 = jnp.bfloat16
NT = (((1,), (1,)), ((), ()))
P2_TYPE = F32
HOP = 3.5
STEP = 0.7


def stage_order(chunks):
    events = []
    for k in range(chunks):
        begin = 2.0 + STEP * k
        events.append((0.3 * k, 0, k))
        for stage in range(1, 5):
            events.append((begin + HOP * stage, stage, k))
    return [(stage, k) for _, stage, k in sorted(events)]


def kernel(
    cfg,
    tokens_ref, gain_ref, gate_hbm, up_hbm, down_hbm, probes_ref,
    basis_ref, stretch_ref,
    gate_w, up_w, down_w,
    slope, act, pushed, tangent, grown_all, acc,
    joined, p1_src, p1_dst, p2_src, p2_dst, whole,
    t1_src, t1_dst, t2_src, t2_dst, t_whole,
    col_src, col_dst, sq1, sq1_in, sq2, scale,
    load_sem, p1_ss, p1_rs, p2_ss, p2_rs, g1_ss, g1_rs, g2_ss, g2_rs,
    col_ss, col_rs, ag_ss, ag_rs, sq1_ss, sq1_rs, sq2_ss, sq2_rs,
):
    N, NZ, NC, K, C, probe_count, token_count, entries = cfg
    G = NZ * NC
    M = probe_count * token_count
    R = M // N
    W = C // N
    RB = M // G
    width = gain_ref.shape[1]
    x, y, z, c = (lax.axis_index(name) for name in ("x", "y", "z", "c"))
    other = 1 - c
    a = x * other + y * c
    b = y * other + x * c
    g = z * NC + c

    def a_peer(d):
        return (lax.rem(x + d * other, N), lax.rem(y + d * c, N), z, c)

    def b_peer(d):
        return (lax.rem(x + d * c, N), lax.rem(y + d * other, N), z, c)

    def col_peer(dz, dc):
        return (x, y, lax.rem(z + dz, NZ), lax.rem(c + dc, NC))

    def plus(v, d, n):
        return lax.rem(v + d, n)

    row_offsets = [(dx, dy) for dx in range(N) for dy in range(N) if dx or dy]
    col_offsets = [(dz, dc) for dz in range(NZ) for dc in range(NC) if dz or dc]

    def remote(src, dst, send, recv, device):
        return pltpu.make_async_remote_copy(
            src_ref=src, dst_ref=dst, send_sem=send, recv_sem=recv,
            device_id=device, device_id_type=MESH,
        )

    loads = [
        pltpu.make_async_copy(hbm, vmem, load_sem.at[i])
        for i, (hbm, vmem) in enumerate(((gate_hbm, gate_w), (up_hbm, up_w), (down_hbm, down_w)))
    ]
    for load in loads:
        load.start()

    barrier = pltpu.get_barrier_semaphore()
    for dx, dy in row_offsets:
        device = (lax.rem(x + dx, N), lax.rem(y + dy, N), z, c)
        pl.semaphore_signal(barrier, inc=1, device_id=device, device_id_type=MESH)
    for dz, dc in col_offsets:
        pl.semaphore_signal(barrier, inc=1, device_id=col_peer(dz, dc), device_id_type=MESH)

    gain = gain_ref[...]
    pushed[...] = (
        (probes_ref[...] * gain[None]).astype(BF16).reshape(G, RB, width)
    )
    scaled = (tokens_ref[...].astype(F32) * gain).astype(BF16)
    scale[...] = jnp.ones_like(scale)

    pl.semaphore_wait(barrier, len(row_offsets) + len(col_offsets))
    loads[0].wait()
    loads[1].wait()

    def row_stages(part, own, src, dst, src2, dst2, gathered, emit, consume):
        def rs_a(k, d):
            return remote(
                src.at[k, plus(a, d, N)], dst.at[k, d - 1],
                p1_ss.at[k, d - 1], p1_rs.at[k, d - 1], a_peer(d),
            )

        def rs_b(k, d):
            return remote(
                src2.at[k, plus(b, d, N)], dst2.at[k, d - 1],
                p2_ss.at[k, d - 1], p2_rs.at[k, d - 1], b_peer(d),
            )

        def ag_b(k, d, sender):
            block = gathered.at[k, a, sender]
            return remote(block, block, g1_ss.at[k, d - 1], g1_rs.at[k, d - 1], b_peer(d))

        def ag_a(k, d, sender):
            block = gathered.at[k, sender]
            return remote(block, block, g2_ss.at[k, d - 1], g2_rs.at[k, d - 1], a_peer(d))

        far_first = sorted(range(1, N), key=lambda d: -min(d, N - d))

        def first(k):
            part(k)
            for d in far_first:
                rs_a(k, d).start()

        def second(k):
            total = own(k).astype(F32)
            for d in far_first[::-1]:
                rs_a(k, d).wait_recv()
                total += dst[k, d - 1].astype(F32)
            for j in range(N):
                src2[k, j] = total[:, j * W : (j + 1) * W].astype(src2.dtype)
            for d in far_first:
                rs_b(k, d).start()

        def third(k):
            total = src2[k, b].astype(F32)
            for d in far_first[::-1]:
                rs_b(k, d).wait_recv()
                total += dst2[k, d - 1].astype(F32)
            gathered[k, a, b] = emit(total).astype(gathered.dtype)
            for d in far_first:
                ag_b(k, d, b).start()

        def fourth(k):
            for d in far_first[::-1]:
                ag_b(k, d, plus(b, N - d, N)).wait_recv()
            for d in far_first:
                ag_a(k, d, a).start()

        def fifth(k):
            for d in far_first[::-1]:
                ag_a(k, d, plus(a, N - d, N)).wait_recv()
            consume(k)

        stages = (first, second, third, fourth, fifth)

        def finish():
            for k in range(K):
                for d in range(1, N):
                    rs_a(k, d).wait_send()
                    rs_b(k, d).wait_send()
                    ag_b(k, d, b).wait_send()
                    ag_a(k, d, a).wait_send()

        return stages, finish

    def run_stages(stages, finish, before_third=None):
        waiting = before_third
        for stage, k in stage_order(K):
            if stage == 2 and waiting is not None:
                waiting()
                waiting = None
            stages[stage](k)
        finish()

    def columns(k):
        return slice(k * C, (k + 1) * C)

    half = N // 2

    def token_part(k):
        gate = jnp.dot(scaled, gate_w[:, columns(k)], preferred_element_type=F32)
        up = jnp.dot(scaled, up_w[:, columns(k)], preferred_element_type=F32)
        t1_src[k, :half] = gate.reshape(half, token_count // half, C)
        t1_src[k, half:] = up.reshape(half, token_count // half, C)

    def token_values(k, lo):
        return jnp.concatenate(
            [
                jnp.concatenate([t_whole[k, i, j] for i in range(lo, lo + half)], axis=0)
                for j in range(N)
            ],
            axis=1,
        )

    def token_use(k):
        gate = token_values(k, 0)
        up = token_values(k, half)
        sigmoid = 1.0 / (1.0 + jnp.exp(-gate))
        act[:, columns(k)] = gate * sigmoid
        slope[:, columns(k)] = sigmoid * (1.0 + gate * (1.0 - sigmoid)) * up

    run_stages(
        *row_stages(
            token_part, lambda k: t1_src[k, a], t1_src, t1_dst, t2_src, t2_dst, t_whole,
            lambda total: total, token_use,
        )
    )
    loads[2].wait()

    def by_token(values, factor):
        return (values.reshape(probe_count, token_count, C) * factor[None]).reshape(M, C)

    def send_joined(k, value):
        blocks = value.reshape(N, R, C)
        joined[k] = blocks
        p1_src[k] = blocks.astype(BF16)

    def chunk_rows(k):
        return jnp.concatenate(
            [whole[k, :, j].reshape(M, W) for j in range(N)], axis=1
        )

    def hidden_part(k):
        lhs = pushed[...].reshape(M, width)
        gate_tan = jnp.dot(lhs, gate_w[:, columns(k)], preferred_element_type=F32)
        up_tan = jnp.dot(lhs, up_w[:, columns(k)], preferred_element_type=F32)
        send_joined(k, by_token(gate_tan, slope[:, columns(k)]) + by_token(up_tan, act[:, columns(k)]))

    def add_to_acc(k, value):
        acc[...] = value if k == 0 else acc[...] + value

    def hidden_use(k):
        add_to_acc(k, jnp.dot(chunk_rows(k), down_w[columns(k), :], preferred_element_type=F32))

    def back_part(k):
        lhs = tangent[...].reshape(M, width)
        send_joined(k, lax.dot_general(lhs, down_w[columns(k), :], NT, preferred_element_type=F32))

    def back_use(k):
        piece = chunk_rows(k).astype(F32)
        gate_pull = by_token(piece, slope[:, columns(k)]).astype(BF16)
        up_pull = by_token(piece, act[:, columns(k)]).astype(BF16)
        value = lax.dot_general(gate_pull, gate_w[:, columns(k)], NT, preferred_element_type=F32)
        value += lax.dot_general(up_pull, up_w[:, columns(k)], NT, preferred_element_type=F32)
        add_to_acc(k, value)

    def col_index(dz, dc):
        return lax.rem(z + dz, NZ) * NC + lax.rem(c + dc, NC)

    def col_from(dz, dc):
        return lax.rem(z + NZ - dz, NZ) * NC + lax.rem(c + NC - dc, NC)

    def col_reduced(which):
        col_src[which] = acc[...].reshape(G, RB, width)

        def copy(slot, dz, dc):
            return remote(
                col_src.at[which, col_index(dz, dc)], col_dst.at[which, slot],
                col_ss.at[which, slot], col_rs.at[which, slot], col_peer(dz, dc),
            )

        copies = [copy(slot, dz, dc) for slot, (dz, dc) in enumerate(col_offsets)]
        for cp in copies[::-1]:
            cp.start()
        total = col_src[which, g]
        for slot, cp in enumerate(copies):
            cp.wait_recv()
            total += col_dst[which, slot]
        for cp in copies:
            cp.wait_send()
        return total

    def col_gather(buffer, sems):
        send, recv = ag_ss.at[sems], ag_rs.at[sems]

        def copy(slot, dz, dc, owner):
            return remote(buffer.at[owner], buffer.at[owner], send.at[slot], recv.at[slot], col_peer(dz, dc))

        for slot, (dz, dc) in reversed(list(enumerate(col_offsets))):
            copy(slot, dz, dc, g).start()

        def finish():
            for slot, (dz, dc) in enumerate(col_offsets):
                copy(slot, dz, dc, col_from(dz, dc)).wait_recv()
            for slot, (dz, dc) in enumerate(col_offsets):
                copy(slot, dz, dc, g).wait_send()

        return finish

    def fold(values):
        rows, lanes = values.shape
        total = None
        for r in range(0, rows, 8):
            for l in range(0, lanes, 128):
                piece = values[r : r + 8, l : l + 128]
                total = piece if total is None else total + piece
        return total

    def square_copies():
        return [
            remote(
                sq1, sq1_in.at[slot], sq1_ss.at[slot], sq1_rs.at[slot],
                (lax.rem(x + dx, N), lax.rem(y + dy, N), z, c),
            )
            for slot, (dx, dy) in enumerate(row_offsets)
        ]

    def level_copy(slot, dz, dc, owner):
        return remote(sq2.at[owner], sq2.at[owner], sq2_ss.at[slot], sq2_rs.at[slot], col_peer(dz, dc))

    def squares_over_row():
        copies = square_copies()
        total = sq1[...]
        for slot, cp in enumerate(copies):
            cp.wait_recv()
            total += sq1_in[slot]
        for cp in copies:
            cp.wait_send()
        sq2[g] = total
        for slot, (dz, dc) in reversed(list(enumerate(col_offsets))):
            level_copy(slot, dz, dc, g).start()

    def squares_over_col():
        for slot, (dz, dc) in enumerate(col_offsets):
            level_copy(slot, dz, dc, col_from(dz, dc)).wait_recv()
            level_copy(slot, dz, dc, g).wait_send()

    owners = token_count // RB

    def level_of(probe):
        total = sq2[probe * owners]
        for i in range(1, owners):
            total += sq2[probe * owners + i]
        return jnp.sum(jnp.sum(total, axis=0, keepdims=True), axis=1, keepdims=True) / entries

    def sweep(it, carry):
        def norms():
            @pl.when(it > 0)
            def _():
                squares_over_row()

        run_stages(
            *row_stages(
                hidden_part, lambda k: joined[k, a], p1_src, p1_dst, p2_src, p2_dst, whole,
                lambda total: total, hidden_use,
            ),
            before_third=norms,
        )

        @pl.when(it > 0)
        def _():
            squares_over_col()
            factor = lax.rsqrt(level_of(g // owners) + EPSILON)
            scale[...] = jnp.broadcast_to(factor, scale.shape)

        total = col_reduced(0)
        tangent[g] = (total * scale[0:1, 0:1]).astype(BF16)
        col_gather(tangent, 0)()

        run_stages(
            *row_stages(
                back_part, lambda k: joined[k, a], p1_src, p1_dst, p2_src, p2_dst, whole,
                lambda total: total, back_use,
            )
        )
        grown = col_reduced(1) * gain
        grown_all[g] = grown
        sq1[...] = fold(grown * grown)
        for cp in square_copies():
            cp.start()

        @pl.when(it < ITERS - 1)
        def _():
            pushed[g] = (grown * gain).astype(BF16)
            col_gather(pushed, 1)()

        return carry

    lax.fori_loop(0, ITERS, sweep, 0)

    wait_grown = col_gather(grown_all, 2)
    squares_over_row()
    wait_grown()
    squares_over_col()
    lane = lax.broadcasted_iota(jnp.int32, (1, probe_count), 1)
    stretch = jnp.zeros((1, probe_count), F32)
    per = G // probe_count
    for p in range(probe_count):
        level = level_of(p)
        stretch = jnp.where(lane == p, jnp.sqrt(level), stretch)
        rows = jnp.concatenate([grown_all[p * per + i] for i in range(per)], axis=0)
        basis_ref[p] = rows * lax.rsqrt(level + EPSILON)
    stretch_ref[...] = stretch


def solution(mesh, chunk=512, shape=(4, 4, 4, 2)):
    N, _, NZ, NC = shape
    torus = Mesh(mesh.devices.reshape(shape), ("x", "y", "z", "c"))
    row, col = ("x", "y"), ("z", "c")

    def local(tokens, gain, gate_weight, up_weight, down_weight, probes):
        probe_count, token_count, width = probes.shape
        hidden = gate_weight.shape[1]
        M = probe_count * token_count
        G = NZ * NC
        K, C = hidden // chunk, chunk
        R, W, RB = M // N, C // N, M // G
        TR = 2 * token_count // N
        entries = token_count * width * N * N
        cfg = (N, NZ, NC, K, C, probe_count, token_count, entries)
        vm = pltpu.VMEM
        dma = pltpu.SemaphoreType.DMA
        basis, stretch = pl.pallas_call(
            functools.partial(kernel, cfg),
            out_shape=(
                jax.ShapeDtypeStruct(probes.shape, F32),
                jax.ShapeDtypeStruct((1, probe_count), F32),
            ),
            in_specs=[
                pl.BlockSpec(memory_space=pltpu.VMEM),
                pl.BlockSpec(memory_space=pltpu.VMEM),
                pl.BlockSpec(memory_space=pl.ANY),
                pl.BlockSpec(memory_space=pl.ANY),
                pl.BlockSpec(memory_space=pl.ANY),
                pl.BlockSpec(memory_space=pltpu.VMEM),
            ],
            out_specs=(
                pl.BlockSpec(memory_space=pltpu.VMEM),
                pl.BlockSpec(memory_space=pltpu.VMEM),
            ),
            scratch_shapes=[
                vm((width, hidden), BF16), vm((width, hidden), BF16), vm((hidden, width), BF16),
                vm((token_count, hidden), F32), vm((token_count, hidden), F32),
                vm((G, RB, width), BF16), vm((G, RB, width), BF16), vm((G, RB, width), F32),
                vm((M, width), F32),
                vm((K, N, R, C), F32), vm((K, N, R, C), BF16), vm((K, N - 1, R, C), BF16),
                vm((K, N, R, W), P2_TYPE), vm((K, N - 1, R, W), P2_TYPE), vm((K, N, N, R, W), BF16),
                vm((K, N, TR, C), F32), vm((K, N - 1, TR, C), F32),
                vm((K, N, TR, W), F32), vm((K, N - 1, TR, W), F32), vm((K, N, N, TR, W), F32),
                vm((2, G, RB, width), F32), vm((2, G - 1, RB, width), F32),
                vm((8, 128), F32), vm((N * N - 1, 8, 128), F32), vm((G, 8, 128), F32),
                vm((8, 128), F32),
                dma((3,)),
                *[dma((K, N - 1)) for _ in range(8)],
                dma((2, G - 1)), dma((2, G - 1)),
                dma((3, G - 1)), dma((3, G - 1)),
                dma((N * N - 1,)), dma((N * N - 1,)),
                dma((G - 1,)), dma((G - 1,)),
            ],
            compiler_params=pltpu.CompilerParams(collective_id=0, has_side_effects=True),
        )(tokens, gain.reshape(1, width), gate_weight, up_weight, down_weight, probes)
        return basis, stretch.reshape(probe_count)

    return jax.shard_map(
        local,
        mesh=torus,
        in_specs=(P(None, row), P(row), P(row, col), P(row, col), P(col, row), P(None, None, row)),
        out_specs=(P(None, None, row), P()),
        check_vma=False,
    )
```

time: 656 us -> 234 us (0.36)
  blocking collectives: 490 us -> 0 us
  Pallas kernels: 0 us -> 230 us
  waiting for transfers between devices: 88 us -> 0 us
  matrix products: 41.8 us -> 0 us
  between operations: 14.4 us -> 0.64 us
  local copies, waits for them, and re-layouts: 10.8 us -> 2.8 us
    all_to_all x18 -> x0, blocking collectives: 450 us -> none  [the longest x12 298 us: from_everyone(): return lax.all_to_all(copies, axis, split_axis=0, concat_axis=0, tiled=True)]
    pallas_call x0 -> x1, Pallas kernels: none -> 230 us  [local(): pl.pallas_call(functools.partial(kernel, cfg), out_shape=(jax.ShapeDtypeS...]
    psum x1 -> x0, waiting for transfers between devices: 88 us -> none  [local(): gate, up = lax.psum((gate_part, up_part), ROW)]
    dot_general x20 -> x0, matrix products: 41.8 us -> none  [the longest x3 10 us: local(): lax.dot_general(tangent, down_weight, transposed, preferred_element_type=...]
    psum x6 -> x0, blocking collectives: 40.3 us -> none  [by_axis(): return functools.reduce(lax.psum, axes, array)]
  transfers between devices with their start and end apart: 1 -> 0, of which waited for: 1 -> 0; matrix products, arithmetic and copies ran while one was open for 0% -> 0% of each run, Pallas kernels for 0% -> 0%
where the time goes in v1:
time: 234 us
  Pallas kernels  230 us (98%)
  local copies, waits for them, and re-layouts  2.8 us (1%)
    pallas_call x1, Pallas kernels, local(): pl.pallas_call(functools.partial(kernel, cfg), out_shape=(jax.ShapeDtypeS...  230 us

profile of v1, /device:TPU:1, one launch (start us, length us, event | category | flops | bytes accessed | tf_op | source)
XLA Modules:
  0.0 233.8 jit_solution(11537526758452799591)
XLA Ops:
  0.6 230.3 %shard_map.77 = (f32[4,32,512]{2,1,0:T(8,128)}, f32[1,4]{1,0:T(1,128)}) custom-call(bf16[32,512]{1,0:T(8,128)(2,1)} %tokens_ref.1, f32[1,512]{1,0:T(1,128)} %bitcast.2, bf16[512,3584]{1,0:T(8,128)(2,1)} %gate_hbm.1, bf16[512,3584]{1,0:T(8,128)(2,1)} %up_hbm.1, bf16[3584,512]{1,0:T(8,128)(2,1)} %down_hbm.1, f32[4,32,512]{2,1,0:T(8,128)} %probes_ref.1), custom_call_target="tpu_custom_call" | custom-call | tf_op jit(solution)/shard_map/pallas_call | solution.py:420
  231.0 1.7 copy.10
  232.6 1.1 copy.11

commit v2 on v1

v2 whole, which is shorter than its diff:
```python
import functools

import jax
import jax.numpy as jnp
from jax import lax
from jax.experimental import pallas as pl
from jax.experimental.pallas import tpu as pltpu
from jax.sharding import Mesh
from jax.sharding import PartitionSpec as P

ITERS = 3
EPSILON = 1e-06
MESH = pl.DeviceIdType.MESH
F32 = jnp.float32
BF16 = jnp.bfloat16
NT = (((1,), (1,)), ((), ()))
CHUNK = 512
MODES = (3, 3, 3, 3, 3, 3, 3)
TOKEN_MODES = (3, 3, 3, 3, 3, 3, 3)
TOKEN_TYPES = (BF16, F32, F32)
HOP = 3.0
STEP = 0.8


def stage_order(modes):
    events = []
    for k, mode in enumerate(modes):
        events.append((0.3 * k, 0, k))
        for stage in range(1, mode + 1):
            events.append((1.0 + STEP * (k + 1) + HOP * stage, stage, k))
    return [(stage, k) for _, stage, k in sorted(events)]


def kernel(
    cfg,
    tokens_ref, gain_ref, gate_hbm, up_hbm, down_hbm, probes_ref,
    basis_ref, stretch_ref,
    gate_w, up_w, down_w,
    slope, act, pushed, tangent, grown_all, acc,
    joined, p1_src, p1_dst, p2_src, p2_dst, whole,
    t1_own, t1_src, t1_dst, t2_src, t2_dst, t_whole,
    pair_in, z_src, z_dst, sq, sq_in, scale,
    gate_sem, up_sem, down_sem, p1_ss, p1_rs, p2_ss, p2_rs, g1_ss, g1_rs, g2_ss, g2_rs,
    pair_ss, pair_rs, z_ss, z_rs, sq_ss, sq_rs,
):
    N, NZ, K, C, probe_count, token_count, entries = cfg
    M = probe_count * token_count
    R = M // N
    W = C // N
    half = M // 2
    half_probes = probe_count // 2
    width = gain_ref.shape[1]
    x, y, z, c = (lax.axis_index(name) for name in ("x", "y", "z", "c"))
    other = 1 - c
    a = x * other + y * c
    b = y * other + x * c

    def a_peer(d):
        return (lax.rem(x + d * other, N), lax.rem(y + d * c, N), z, c)

    def b_peer(d):
        return (lax.rem(x + d * c, N), lax.rem(y + d * other, N), z, c)

    def row_peer(dx, dy):
        return (lax.rem(x + dx, N), lax.rem(y + dy, N), z, c)

    def z_peer(d):
        return (x, y, lax.rem(z + d, NZ), c)

    partner = (x, y, z, other)
    row_offsets = [(dx, dy) for dx in range(N) for dy in range(N) if dx or dy]

    def plus(v, d, n):
        return lax.rem(v + d, n)

    def columns(k):
        return slice(k * C, (k + 1) * C)

    def remote(src, dst, send, recv, device):
        return pltpu.make_async_remote_copy(
            src_ref=src, dst_ref=dst, send_sem=send, recv_sem=recv,
            device_id=device, device_id_type=MESH,
        )

    gate_loads = [
        pltpu.make_async_copy(gate_hbm.at[:, columns(k)], gate_w.at[:, columns(k)], gate_sem.at[k])
        for k in range(K)
    ]
    up_loads = [
        pltpu.make_async_copy(up_hbm.at[:, columns(k)], up_w.at[:, columns(k)], up_sem.at[k])
        for k in range(K)
    ]
    down_load = pltpu.make_async_copy(down_hbm, down_w, down_sem.at[0])
    for k in range(K):
        gate_loads[k].start()
        up_loads[k].start()
    down_load.start()

    barrier = pltpu.get_barrier_semaphore()
    greeted = [row_peer(dx, dy) for dx, dy in row_offsets]
    greeted += [z_peer(d) for d in range(1, NZ)] + [partner]
    for device in greeted:
        pl.semaphore_signal(barrier, inc=1, device_id=device, device_id_type=MESH)

    gain = gain_ref[...]
    pushed[...] = (probes_ref[...] * gain[None]).astype(BF16).reshape(2, half, width)
    scaled = (tokens_ref[...].astype(F32) * gain).astype(BF16)
    scale[...] = jnp.ones_like(scale)

    far_first = sorted(range(1, N), key=lambda d: -min(d, N - d))
    near_first = far_first[::-1]

    def row_stages(phase, part, own, modes, src, dst, src2, dst2, gathered, consume):
        def block(j):
            return pl.ds(pl.multiple_of(j * W, W), W)

        def rs_a(k, d):
            return remote(
                src.at[k, plus(a, d, N)], dst.at[k, d - 1],
                p1_ss.at[k, d - 1], p1_rs.at[k, d - 1], a_peer(d),
            )

        def over_b(k, d):
            if modes[k] == 3:
                sent, taken = src2.at[k], dst2.at[k, d - 1]
            else:
                sent, taken = src2.at[k, :, block(plus(b, d, N))], dst2.at[k, d - 1, :, 0:W]
            return remote(sent, taken, p2_ss.at[phase, k, d - 1], p2_rs.at[phase, k, d - 1], b_peer(d))

        def ag_b(k, d, sender):
            piece = gathered.at[k, a, :, block(sender)]
            return remote(piece, piece, g1_ss.at[k, d - 1], g1_rs.at[k, d - 1], b_peer(d))

        def ag_a(k, d, sender):
            piece = gathered.at[k, sender]
            return remote(piece, piece, g2_ss.at[k, d - 1], g2_rs.at[k, d - 1], a_peer(d))

        def first(k):
            part(k)
            for d in far_first:
                rs_a(k, d).start()

        def second(k):
            total = own(k)
            for d in near_first:
                rs_a(k, d).wait_recv()
                total += dst[k, d - 1].astype(F32)
            src2[k] = total.astype(src2.dtype)
            for d in far_first:
                over_b(k, d).start()
            own_sum(k, total)

        def own_sum(k, total):
            kept = joined if src is p1_src else t1_own
            kept[k, a] = total

        def third(k):
            kept = joined if src is p1_src else t1_own
            if modes[k] == 3:
                total = kept[k, a]
                for d in near_first:
                    over_b(k, d).wait_recv()
                    total += dst2[k, d - 1].astype(F32)
                gathered[k, a] = total.astype(gathered.dtype)
                for d in far_first:
                    ag_a(k, d, a).start()
            else:
                total = kept[k, a, :, block(b)]
                for d in near_first:
                    over_b(k, d).wait_recv()
                    total += dst2[k, d - 1, :, 0:W].astype(F32)
                gathered[k, a, :, block(b)] = total.astype(gathered.dtype)
                for d in far_first:
                    ag_b(k, d, b).start()

        def fourth(k):
            for d in near_first:
                ag_b(k, d, plus(b, N - d, N)).wait_recv()
            for d in far_first:
                ag_a(k, d, a).start()

        def last(k):
            for d in near_first:
                ag_a(k, d, plus(a, N - d, N)).wait_recv()
            consume(k)

        def stages_of(k):
            return (first, second, third, last) if modes[k] == 3 else (first, second, third, fourth, last)

        def finish():
            for k in range(K):
                for d in range(1, N):
                    rs_a(k, d).wait_send()
                    over_b(k, d).wait_send()
                    if modes[k] == 4:
                        ag_b(k, d, b).wait_send()
                    ag_a(k, d, a).wait_send()

        for stage, k in stage_order(modes):
            stages_of(k)[stage](k)
        finish()

    halves = N // 2

    def token_compute(k):
        gate_loads[k].wait()
        up_loads[k].wait()
        gate = jnp.dot(scaled, gate_w[:, columns(k)], preferred_element_type=F32)
        up = jnp.dot(scaled, up_w[:, columns(k)], preferred_element_type=F32)
        gate = gate.reshape(halves, token_count // halves, C)
        up = up.reshape(halves, token_count // halves, C)
        t1_own[k, :halves] = gate
        t1_own[k, halves:] = up
        t1_src[k, :halves] = gate.astype(t1_src.dtype)
        t1_src[k, halves:] = up.astype(t1_src.dtype)

    for k in range(K):
        token_compute(k)
    pl.semaphore_wait(barrier, len(greeted))

    def token_use(k):
        gate = t_whole[k, :halves].reshape(token_count, C).astype(F32)
        up = t_whole[k, halves:].reshape(token_count, C).astype(F32)
        sigmoid = 1.0 / (1.0 + jnp.exp(-gate))
        act[:, columns(k)] = gate * sigmoid
        slope[:, columns(k)] = sigmoid * (1.0 + gate * (1.0 - sigmoid)) * up

    row_stages(
        2, lambda k: None, lambda k: t1_own[k, a], TOKEN_MODES,
        t1_src, t1_dst, t2_src, t2_dst, t_whole, token_use,
    )
    down_load.wait()

    def by_token(values, factor):
        return (values.reshape(probe_count, token_count, C) * factor[None]).reshape(M, C)

    def send_joined(k, value):
        blocks = value.reshape(N, R, C)
        joined[k] = blocks
        p1_src[k] = blocks.astype(BF16)

    def hidden_part(k):
        lhs = pushed[...].reshape(M, width)
        gate_tan = jnp.dot(lhs, gate_w[:, columns(k)], preferred_element_type=F32)
        up_tan = jnp.dot(lhs, up_w[:, columns(k)], preferred_element_type=F32)
        send_joined(k, by_token(gate_tan, slope[:, columns(k)]) + by_token(up_tan, act[:, columns(k)]))

    def add_to_acc(k, value):
        value = value.reshape(2, half, width)
        acc[...] = value if k == 0 else acc[...] + value

    def hidden_use(k):
        lhs = whole[k].reshape(M, C)
        add_to_acc(k, jnp.dot(lhs, down_w[columns(k), :], preferred_element_type=F32))

    def back_part(k):
        lhs = tangent[...].reshape(M, width)
        send_joined(k, lax.dot_general(lhs, down_w[columns(k), :], NT, preferred_element_type=F32))

    def back_use(k):
        piece = whole[k].reshape(M, C).astype(F32)
        gate_pull = by_token(piece, slope[:, columns(k)]).astype(BF16)
        up_pull = by_token(piece, act[:, columns(k)]).astype(BF16)
        value = lax.dot_general(gate_pull, gate_w[:, columns(k)], NT, preferred_element_type=F32)
        value += lax.dot_general(up_pull, up_w[:, columns(k)], NT, preferred_element_type=F32)
        add_to_acc(k, value)

    def col_half(phase):
        swap = remote(acc.at[other], pair_in, pair_ss.at[0], pair_rs.at[0], partner)
        swap.start()
        total = acc[c]
        swap.wait_recv()
        total += pair_in[...]
        z_src[...] = total.astype(z_src.dtype)
        copies = [
            remote(z_src, z_dst.at[phase, d - 1], z_ss.at[phase, d - 1], z_rs.at[phase, d - 1], z_peer(d))
            for d in range(1, NZ)
        ]
        for d in sorted(range(1, NZ), key=lambda d: -min(d, NZ - d)):
            copies[d - 1].start()
        acc[c] = total
        swap.wait_send()
        for d in sorted(range(1, NZ), key=lambda d: min(d, NZ - d)):
            copies[d - 1].wait_recv()
        total = acc[c]
        for d in range(1, NZ):
            total += z_dst[phase, d - 1].astype(F32)
        for cp in copies:
            cp.wait_send()
        return total

    def share(buffer, which):
        mine, theirs = buffer.at[c], buffer.at[other]
        send, recv = pair_ss.at[which], pair_rs.at[which]
        remote(mine, mine, send, recv, partner).start()
        remote(theirs, theirs, send, recv, partner).wait_recv()
        remote(mine, mine, send, recv, partner).wait_send()

    def folded(values):
        rows, lanes = values.shape
        total = None
        for r in range(0, rows, 8):
            for l in range(0, lanes, 128):
                piece = values[r : r + 8, l : l + 128]
                total = piece if total is None else total + piece
        return jnp.sum(total, axis=0, keepdims=True)

    def square_copies():
        return [
            remote(sq, sq_in.at[slot], sq_ss.at[slot], sq_rs.at[slot], row_peer(dx, dy))
            for slot, (dx, dy) in enumerate(row_offsets)
        ]

    def send_squares():
        for p in range(probe_count):
            i, j = divmod(p, half_probes)
            values = grown_all[i, j * token_count : (j + 1) * token_count]
            sq[p : p + 1] = folded(values * values)
        for cp in square_copies():
            cp.start()

    def levels():
        total = sq[...]
        copies = square_copies()
        for cp in copies:
            cp.wait_recv()
        for slot in range(len(copies)):
            total += sq_in[slot]
        for cp in copies:
            cp.wait_send()
        return jnp.sum(total, axis=1, keepdims=True) / entries

    def sweep(it, carry):
        row_stages(
            0, hidden_part, lambda k: joined[k, a], MODES, p1_src, p1_dst, p2_src, p2_dst.at[0], whole, hidden_use,
        )
        total = col_half(0)

        @pl.when(it > 0)
        def _():
            factor = lax.rsqrt(levels() + EPSILON)
            for p in range(probe_count):
                scale[p] = jnp.broadcast_to(factor[p : p + 1], scale.shape[1:])

        parts = [
            total[i * token_count : (i + 1) * token_count] * scale[c * half_probes + i, 0:1, 0:1]
            for i in range(half_probes)
        ]
        tangent[c] = jnp.concatenate(parts, axis=0).astype(BF16)
        share(tangent, 1)

        row_stages(
            1, back_part, lambda k: joined[k, a], MODES, p1_src, p1_dst, p2_src, p2_dst.at[1], whole, back_use,
        )
        grown_all[c] = col_half(1) * gain
        share(grown_all, 2)
        send_squares()
        pushed[...] = (grown_all[...] * gain[None]).astype(BF16)
        return carry

    sq[...] = jnp.zeros_like(sq)
    lax.fori_loop(0, ITERS, sweep, 0)

    level = levels()
    root = jnp.sqrt(level)
    factor = lax.rsqrt(level + EPSILON)
    lane = lax.broadcasted_iota(jnp.int32, (1, probe_count), 1)
    stretch = jnp.zeros((1, probe_count), F32)
    for p in range(probe_count):
        stretch = jnp.where(lane == p, root[p : p + 1], stretch)
        i, j = divmod(p, half_probes)
        basis_ref[p] = grown_all[i, j * token_count : (j + 1) * token_count] * factor[p : p + 1]
    stretch_ref[...] = stretch


def solution(mesh, chunk=CHUNK, shape=(4, 4, 4, 2)):
    N, _, NZ, _ = shape
    torus = Mesh(mesh.devices.reshape(shape), ("x", "y", "z", "c"))
    row, col = ("x", "y"), ("z", "c")

    def local(tokens, gain, gate_weight, up_weight, down_weight, probes):
        probe_count, token_count, width = probes.shape
        hidden = gate_weight.shape[1]
        M = probe_count * token_count
        K, C = hidden // chunk, chunk
        R = M // N
        TR = 2 * token_count // N
        T1, T2, TG = TOKEN_TYPES
        entries = token_count * width * N * N
        cfg = (N, NZ, K, C, probe_count, token_count, entries)
        vm = pltpu.VMEM
        dma = pltpu.SemaphoreType.DMA
        basis, stretch = pl.pallas_call(
            functools.partial(kernel, cfg),
            out_shape=(
                jax.ShapeDtypeStruct(probes.shape, F32),
                jax.ShapeDtypeStruct((1, probe_count), F32),
            ),
            in_specs=[
                pl.BlockSpec(memory_space=pltpu.VMEM),
                pl.BlockSpec(memory_space=pltpu.VMEM),
                pl.BlockSpec(memory_space=pl.ANY),
                pl.BlockSpec(memory_space=pl.ANY),
                pl.BlockSpec(memory_space=pl.ANY),
                pl.BlockSpec(memory_space=pltpu.VMEM),
            ],
            out_specs=(
                pl.BlockSpec(memory_space=pltpu.VMEM),
                pl.BlockSpec(memory_space=pltpu.VMEM),
            ),
            scratch_shapes=[
                vm((width, hidden), BF16), vm((width, hidden), BF16), vm((hidden, width), BF16),
                vm((token_count, hidden), F32), vm((token_count, hidden), F32),
                vm((2, M // 2, width), BF16), vm((2, M // 2, width), BF16), vm((2, M // 2, width), F32),
                vm((2, M // 2, width), F32),
                vm((K, N, R, C), F32), vm((K, N, R, C), BF16), vm((K, N - 1, R, C), BF16),
                vm((K, R, C), BF16), vm((2, K, N - 1, R, C), BF16), vm((K, N, R, C), BF16),
                vm((K, N, TR, C), F32), vm((K, N, TR, C), T1), vm((K, N - 1, TR, C), T1),
                vm((K, TR, C), T2), vm((K, N - 1, TR, C), T2), vm((K, N, TR, C), TG),
                vm((M // 2, width), F32), vm((M // 2, width), BF16), vm((2, NZ - 1, M // 2, width), BF16),
                vm((8, 128), F32), vm((N * N - 1, 8, 128), F32),
                vm((probe_count, 8, 128), F32),
                dma((K,)), dma((K,)), dma((1,)),
                dma((K, N - 1)), dma((K, N - 1)), dma((3, K, N - 1)), dma((3, K, N - 1)),
                *[dma((K, N - 1)) for _ in range(4)],
                dma((3,)), dma((3,)),
                dma((2, NZ - 1)), dma((2, NZ - 1)),
                dma((N * N - 1,)), dma((N * N - 1,)),
            ],
            compiler_params=pltpu.CompilerParams(collective_id=0, has_side_effects=True),
        )(tokens, gain.reshape(1, width), gate_weight, up_weight, down_weight, probes)
        return basis, stretch.reshape(probe_count)

    return jax.shard_map(
        local,
        mesh=torus,
        in_specs=(P(None, row), P(row), P(row, col), P(row, col), P(col, row), P(None, None, row)),
        out_specs=(P(None, None, row), P()),
        check_vma=False,
    )
```

time: 234 us -> 204 us (0.87)
  Pallas kernels: 230 us -> 201 us
    pallas_call x1, Pallas kernels: 230 us -> 201 us  [local(): pl.pallas_call(functools.partial(kernel, cfg), out_shape=(jax.ShapeDtypeS...]
where the time goes in v2:
time: 204 us
  Pallas kernels  201 us (99%)
  local copies, waits for them, and re-layouts  2.8 us (1%)
    pallas_call x1, Pallas kernels, local(): pl.pallas_call(functools.partial(kernel, cfg), out_shape=(jax.ShapeDtypeS...  201 us

profile of v2, /device:TPU:1, one launch (start us, length us, event | category | flops | bytes accessed | tf_op | source)
XLA Modules:
  0.0 204.1 jit_solution(18306970677151015324)
XLA Ops:
  0.6 200.7 %shard_map.77 = (f32[4,32,512]{2,1,0:T(8,128)}, f32[1,4]{1,0:T(1,128)}) custom-call(bf16[32,512]{1,0:T(8,128)(2,1)} %tokens_ref.1, f32[1,512]{1,0:T(1,128)} %bitcast.2, bf16[512,3584]{1,0:T(8,128)(2,1)} %gate_hbm.1, bf16[512,3584]{1,0:T(8,128)(2,1)} %up_hbm.1, bf16[3584,512]{1,0:T(8,128)(2,1)} %down_hbm.1, f32[4,32,512]{2,1,0:T(8,128)} %probes_ref.1), custom_call_target="tpu_custom_call" | custom-call | tf_op jit(solution)/shard_map/pallas_call | solution.py:393
  201.3 1.7 copy.10
  203.0 1.1 copy.11

commit v3 on v2

--- a/solution.py
+++ b/solution.py
@@ -19,7 +19,7 @@
 TOKEN_MODES = (3, 3, 3, 3, 3, 3, 3)
 TOKEN_TYPES = (BF16, F32, F32)
 HOP = 3.0
-STEP = 0.8
+STEP = 0.5
 
 
 def stage_order(modes):
@@ -52,14 +52,21 @@
     width = gain_ref.shape[1]
     x, y, z, c = (lax.axis_index(name) for name in ("x", "y", "z", "c"))
     other = 1 - c
-    a = x * other + y * c
-    b = y * other + x * c
-
-    def a_peer(d):
-        return (lax.rem(x + d * other, N), lax.rem(y + d * c, N), z, c)
-
-    def b_peer(d):
-        return (lax.rem(x + d * c, N), lax.rem(y + d * other, N), z, c)
+    swaps = (c, other)
+    a_at = (x * other + y * c, y * other + x * c)
+
+    def a_of(k):
+        return a_at[k % 2]
+
+    def b_of(k):
+        return a_at[1 - k % 2]
+
+    def a_peer(k, d):
+        swap = swaps[k % 2]
+        return (lax.rem(x + d * (1 - swap), N), lax.rem(y + d * swap, N), z, c)
+
+    def b_peer(k, d):
+        return a_peer(k + 1, d)
 
     def row_peer(dx, dy):
         return (lax.rem(x + dx, N), lax.rem(y + dy, N), z, c)
@@ -116,24 +123,24 @@
 
         def rs_a(k, d):
             return remote(
-                src.at[k, plus(a, d, N)], dst.at[k, d - 1],
-                p1_ss.at[k, d - 1], p1_rs.at[k, d - 1], a_peer(d),
+                src.at[k, plus(a_of(k), d, N)], dst.at[k, d - 1],
+                p1_ss.at[k, d - 1], p1_rs.at[k, d - 1], a_peer(k, d),
             )
 
         def over_b(k, d):
             if modes[k] == 3:
                 sent, taken = src2.at[k], dst2.at[k, d - 1]
             else:
-                sent, taken = src2.at[k, :, block(plus(b, d, N))], dst2.at[k, d - 1, :, 0:W]
-            return remote(sent, taken, p2_ss.at[phase, k, d - 1], p2_rs.at[phase, k, d - 1], b_peer(d))
+                sent, taken = src2.at[k, :, block(plus(b_of(k), d, N))], dst2.at[k, d - 1, :, 0:W]
+            return remote(sent, taken, p2_ss.at[phase, k, d - 1], p2_rs.at[phase, k, d - 1], b_peer(k, d))
 
         def ag_b(k, d, sender):
-            piece = gathered.at[k, a, :, block(sender)]
-            return remote(piece, piece, g1_ss.at[k, d - 1], g1_rs.at[k, d - 1], b_peer(d))
+            piece = gathered.at[k, a_of(k), :, block(sender)]
+            return remote(piece, piece, g1_ss.at[k, d - 1], g1_rs.at[k, d - 1], b_peer(k, d))
 
         def ag_a(k, d, sender):
             piece = gathered.at[k, sender]
-            return remote(piece, piece, g2_ss.at[k, d - 1], g2_rs.at[k, d - 1], a_peer(d))
+            return remote(piece, piece, g2_ss.at[k, d - 1], g2_rs.at[k, d - 1], a_peer(k, d))
 
         def first(k):
             part(k)
@@ -152,36 +159,36 @@
 
         def own_sum(k, total):
             kept = joined if src is p1_src else t1_own
-            kept[k, a] = total
+            kept[k, a_of(k)] = total
 
         def third(k):
             kept = joined if src is p1_src else t1_own
             if modes[k] == 3:
-                total = kept[k, a]
+                total = kept[k, a_of(k)]
                 for d in near_first:
                     over_b(k, d).wait_recv()
                     total += dst2[k, d - 1].astype(F32)
-                gathered[k, a] = total.astype(gathered.dtype)
+                gathered[k, a_of(k)] = total.astype(gathered.dtype)
                 for d in far_first:
-                    ag_a(k, d, a).start()
+                    ag_a(k, d, a_of(k)).start()
             else:
-                total = kept[k, a, :, block(b)]
+                total = kept[k, a_of(k), :, block(b_of(k))]
                 for d in near_first:
                     over_b(k, d).wait_recv()
                     total += dst2[k, d - 1, :, 0:W].astype(F32)
-                gathered[k, a, :, block(b)] = total.astype(gathered.dtype)
+                gathered[k, a_of(k), :, block(b_of(k))] = total.astype(gathered.dtype)
                 for d in far_first:
-                    ag_b(k, d, b).start()
+                    ag_b(k, d, b_of(k)).start()
 
         def fourth(k):
             for d in near_first:
-                ag_b(k, d, plus(b, N - d, N)).wait_recv()
+                ag_b(k, d, plus(b_of(k), N - d, N)).wait_recv()
             for d in far_first:
-                ag_a(k, d, a).start()
+                ag_a(k, d, a_of(k)).start()
 
         def last(k):
             for d in near_first:
-                ag_a(k, d, plus(a, N - d, N)).wait_recv()
+                ag_a(k, d, plus(a_of(k), N - d, N)).wait_recv()
             consume(k)
 
         def stages_of(k):
@@ -193,8 +200,8 @@
                     rs_a(k, d).wait_send()
                     over_b(k, d).wait_send()
                     if modes[k] == 4:
-                        ag_b(k, d, b).wait_send()
-                    ag_a(k, d, a).wait_send()
+                        ag_b(k, d, b_of(k)).wait_send()
+                    ag_a(k, d, a_of(k)).wait_send()
 
         for stage, k in stage_order(modes):
             stages_of(k)[stage](k)
@@ -226,7 +233,7 @@
         slope[:, columns(k)] = sigmoid * (1.0 + gate * (1.0 - sigmoid)) * up
 
     row_stages(
-        2, lambda k: None, lambda k: t1_own[k, a], TOKEN_MODES,
+        2, lambda k: None, lambda k: t1_own[k, a_of(k)], TOKEN_MODES,
         t1_src, t1_dst, t2_src, t2_dst, t_whole, token_use,
     )
     down_load.wait()
@@ -332,7 +339,7 @@
 
     def sweep(it, carry):
         row_stages(
-            0, hidden_part, lambda k: joined[k, a], MODES, p1_src, p1_dst, p2_src, p2_dst.at[0], whole, hidden_use,
+            0, hidden_part, lambda k: joined[k, a_of(k)], MODES, p1_src, p1_dst, p2_src, p2_dst.at[0], whole, hidden_use,
         )
         total = col_half(0)
 
@@ -350,7 +357,7 @@
         share(tangent, 1)
 
         row_stages(
-            1, back_part, lambda k: joined[k, a], MODES, p1_src, p1_dst, p2_src, p2_dst.at[1], whole, back_use,
+            1, back_part, lambda k: joined[k, a_of(k)], MODES, p1_src, p1_dst, p2_src, p2_dst.at[1], whole, back_use,
         )
         grown_all[c] = col_half(1) * gain
         share(grown_all, 2)

time: 204 us -> 193 us (0.946)
  Pallas kernels: 201 us -> 189 us
    pallas_call x1, Pallas kernels: 201 us -> 189 us  [local(): pl.pallas_call(functools.partial(kernel, cfg), out_shape=(jax.ShapeDtypeS...]
where the time goes in v3:
time: 193 us
  Pallas kernels  189 us (98%)
  local copies, waits for them, and re-layouts  2.8 us (1%)
    pallas_call x1, Pallas kernels, local(): pl.pallas_call(functools.partial(kernel, cfg), out_shape=(jax.ShapeDtypeS...  189 us

profile of v3, /device:TPU:1, one launch (start us, length us, event | category | flops | bytes accessed | tf_op | source)
XLA Modules:
  0.0 192.6 jit_solution(10969752548583317877)
XLA Ops:
  0.6 189.2 %shard_map.77 = (f32[4,32,512]{2,1,0:T(8,128)}, f32[1,4]{1,0:T(1,128)}) custom-call(bf16[32,512]{1,0:T(8,128)(2,1)} %tokens_ref.1, f32[1,512]{1,0:T(1,128)} %bitcast.2, bf16[512,3584]{1,0:T(8,128)(2,1)} %gate_hbm.1, bf16[512,3584]{1,0:T(8,128)(2,1)} %up_hbm.1, bf16[3584,512]{1,0:T(8,128)(2,1)} %down_hbm.1, f32[4,32,512]{2,1,0:T(8,128)} %probes_ref.1), custom_call_target="tpu_custom_call" | custom-call | tf_op jit(solution)/shard_map/pallas_call | solution.py:400
  189.8 1.7 copy.10
  191.5 1.1 copy.11

commit v4 on v3

v4 whole, which is shorter than its diff:
```python
import functools

import jax
import jax.numpy as jnp
from jax import lax
from jax.experimental import pallas as pl
from jax.experimental.pallas import tpu as pltpu
from jax.sharding import Mesh
from jax.sharding import PartitionSpec as P

ITERS = 3
EPSILON = 1e-06
MESH = pl.DeviceIdType.MESH
F32 = jnp.float32
BF16 = jnp.bfloat16
NT = (((1,), (1,)), ((), ()))
CHUNK = 512
MODES = (3, 3, 3, 3, 3, 3, 3)
TOKEN_MODES = (3, 3, 3, 3, 3, 3, 3)
TOKEN_TYPES = (BF16, F32, F32)
HOP = 3.0
STEP = 0.5


def stage_order(modes):
    events = []
    for k, mode in enumerate(modes):
        events.append((0.3 * k, 0, k))
        for stage in range(1, mode + 1):
            events.append((1.0 + STEP * (k + 1) + HOP * stage, stage, k))
    return [(stage, k) for _, stage, k in sorted(events)]


def kernel(
    cfg,
    tokens_hbm, gain_hbm, gate_hbm, up_hbm, down_hbm, probes_hbm,
    grown_hbm, level_ref,
    tokens_ref, gain_ref, probes_ref, gate_w, up_w, down_w,
    slope, act, pushed, tangent, grown_all, acc,
    joined, p1_src, p1_dst, p2_src, p2_dst, whole,
    t1_own, t1_src, t1_dst, t2_src, t2_dst, t_whole,
    pair_in, z_src, z_dst, sq, sq_in, scale,
    small_sem, gate_sem, up_sem, down_sem, p1_ss, p1_rs, p2_ss, p2_rs, g1_ss, g1_rs, g2_ss, g2_rs,
    pair_ss, pair_rs, z_ss, z_rs, sq_ss, sq_rs,
):
    N, NZ, K, C, probe_count, token_count, entries = cfg
    M = probe_count * token_count
    R = M // N
    W = C // N
    half = M // 2
    half_probes = probe_count // 2
    width = gain_ref.shape[1]
    x, y, z, c = (lax.axis_index(name) for name in ("x", "y", "z", "c"))
    other = 1 - c
    def around(v, n):
        return [v] + [lax.rem(v + d, n) for d in range(1, n)]

    xs, ys, zs = around(x, N), around(y, N), around(z, NZ)

    def device(i, j, k, core):
        return (i, j, k, core)

    a_at = (
        [xs[d] * other + ys[d] * c for d in range(N)],
        [ys[d] * other + xs[d] * c for d in range(N)],
    )
    a_devices = (
        [device(xs[d] * other + x * c, y * other + ys[d] * c, z, c) for d in range(N)],
        [device(xs[d] * c + x * other, y * c + ys[d] * other, z, c) for d in range(N)],
    )

    def a_of(k, d=0):
        return a_at[k % 2][d]

    def b_of(k, d=0):
        return a_at[1 - k % 2][d]

    def a_peer(k, d):
        return a_devices[k % 2][d]

    def b_peer(k, d):
        return a_devices[1 - k % 2][d]

    def row_peer(dx, dy):
        return device(xs[dx], ys[dy], z, c)

    z_peers = [device(x, y, zs[d], c) for d in range(NZ)]
    partner = device(x, y, z, other)
    row_offsets = [(dx, dy) for dx in range(N) for dy in range(N) if dx or dy]

    def columns(k):
        return slice(k * C, (k + 1) * C)

    def remote(src, dst, send, recv, target):
        return pltpu.make_async_remote_copy(
            src_ref=src, dst_ref=dst, send_sem=send, recv_sem=recv,
            device_id=target, device_id_type=MESH,
        )

    def wait_for(ref, sem):
        pltpu.make_async_copy(ref, ref, sem).wait()

    gate_loads = [
        pltpu.make_async_copy(gate_hbm.at[:, columns(k)], gate_w.at[:, columns(k)], gate_sem.at[k])
        for k in range(K)
    ]
    up_loads = [
        pltpu.make_async_copy(up_hbm.at[:, columns(k)], up_w.at[:, columns(k)], up_sem.at[k])
        for k in range(K)
    ]
    down_load = pltpu.make_async_copy(down_hbm, down_w, down_sem.at[0])
    tokens_load = pltpu.make_async_copy(tokens_hbm, tokens_ref, small_sem.at[0])
    gain_load = pltpu.make_async_copy(gain_hbm, gain_ref, small_sem.at[1])
    probes_load = pltpu.make_async_copy(probes_hbm, probes_ref, small_sem.at[2])
    tokens_load.start()
    gain_load.start()
    for k in range(K):
        gate_loads[k].start()
        up_loads[k].start()
    probes_load.start()
    down_load.start()

    barrier = pltpu.get_barrier_semaphore()
    greeted = [row_peer(dx, dy) for dx, dy in row_offsets]
    greeted += [z_peers[d] for d in range(1, NZ)] + [partner]
    for target in greeted:
        pl.semaphore_signal(barrier, inc=1, device_id=target, device_id_type=MESH)

    tokens_load.wait()
    gain_load.wait()
    gain = gain_ref[...]
    scaled = (tokens_ref[...].astype(F32) * gain).astype(BF16)

    far_first = sorted(range(1, N), key=lambda d: -min(d, N - d))
    near_first = far_first[::-1]

    def row_stages(phase, part, modes, src, dst, src2, dst2, gathered, consume, after_first=None):
        def block(j):
            return pl.ds(pl.multiple_of(j * W, W), W)

        def rs_a(k, d):
            return remote(src.at[k, a_of(k, d)], dst.at[k, d - 1], p1_ss.at[0], p1_rs.at[k], a_peer(k, d))

        def over_b(k, d):
            if modes[k] == 3:
                sent, taken = src2.at[k], dst2.at[k, d - 1]
            else:
                sent, taken = src2.at[k, :, block(b_of(k, d))], dst2.at[k, d - 1, :, 0:W]
            return remote(sent, taken, p2_ss.at[0], p2_rs.at[phase, k], b_peer(k, d))

        def ag_b(k, d):
            piece = gathered.at[k, a_of(k), :, block(b_of(k))]
            return remote(piece, piece, g1_ss.at[0], g1_rs.at[k], b_peer(k, d))

        def ag_a(k, d):
            piece = gathered.at[k, a_of(k)]
            return remote(piece, piece, g2_ss.at[0], g2_rs.at[k], a_peer(k, d))

        def first(k):
            part(k)
            for d in far_first:
                rs_a(k, d).start()

        kept = joined if src is p1_src else t1_own

        def second(k):
            wait_for(dst.at[k], p1_rs.at[k])
            total = kept[k, a_of(k)]
            for d in near_first:
                total += dst[k, d - 1].astype(F32)
            src2[k] = total.astype(src2.dtype)
            for d in far_first:
                over_b(k, d).start()
            kept[k, a_of(k)] = total

        def third(k):
            if modes[k] == 3:
                wait_for(dst2.at[k], p2_rs.at[phase, k])
                total = kept[k, a_of(k)]
                for d in near_first:
                    total += dst2[k, d - 1].astype(F32)
                gathered[k, a_of(k)] = total.astype(gathered.dtype)
                for d in far_first:
                    ag_a(k, d).start()
            else:
                wait_for(dst2.at[k, :, :, 0:W], p2_rs.at[phase, k])
                total = kept[k, a_of(k), :, block(b_of(k))]
                for d in near_first:
                    total += dst2[k, d - 1, :, 0:W].astype(F32)
                gathered[k, a_of(k), :, block(b_of(k))] = total.astype(gathered.dtype)
                for d in far_first:
                    ag_b(k, d).start()

        def fourth(k):
            wait_for(gathered.at[k, a_of(k), :, 0 : (N - 1) * W], g1_rs.at[k])
            for d in far_first:
                ag_a(k, d).start()

        def last(k):
            wait_for(gathered.at[k, 0 : N - 1], g2_rs.at[k])
            consume(k)

        def stages_of(k):
            return (first, second, third, last) if modes[k] == 3 else (first, second, third, fourth, last)

        wide = [k for k in range(K) if modes[k] == 3]
        narrow = [k for k in range(K) if modes[k] == 4]

        def finish():
            wait_for(dst, p1_ss.at[0])
            if narrow:
                wait_for(dst2.at[0 : len(narrow), :, :, 0:W], p2_ss.at[0])
                wait_for(gathered.at[0 : len(narrow), 0 : N - 1, :, 0:W], g1_ss.at[0])
            if wide:
                wait_for(dst2.at[0 : len(wide)], p2_ss.at[0])
            wait_for(gathered.at[:, 0 : N - 1], g2_ss.at[0])

        hook = after_first
        for stage, k in stage_order(modes):
            if stage and hook is not None:
                hook()
                hook = None
            stages_of(k)[stage](k)
        return finish

    halves = N // 2

    def token_compute(k):
        gate_loads[k].wait()
        up_loads[k].wait()
        gate = jnp.dot(scaled, gate_w[:, columns(k)], preferred_element_type=F32)
        up = jnp.dot(scaled, up_w[:, columns(k)], preferred_element_type=F32)
        gate = gate.reshape(halves, token_count // halves, C)
        up = up.reshape(halves, token_count // halves, C)
        t1_own[k, :halves] = gate
        t1_own[k, halves:] = up
        t1_src[k, :halves] = gate.astype(t1_src.dtype)
        t1_src[k, halves:] = up.astype(t1_src.dtype)

    for k in range(K):
        token_compute(k)
    pl.semaphore_wait(barrier, len(greeted))

    def token_use(k):
        gate = t_whole[k, :halves].reshape(token_count, C).astype(F32)
        up = t_whole[k, halves:].reshape(token_count, C).astype(F32)
        sigmoid = 1.0 / (1.0 + jnp.exp(-gate))
        act[:, columns(k)] = gate * sigmoid
        slope[:, columns(k)] = sigmoid * (1.0 + gate * (1.0 - sigmoid)) * up

    def start_probes():
        probes_load.wait()
        pushed[...] = (probes_ref[...] * gain[None]).astype(BF16).reshape(2, half, width)
        scale[...] = jnp.ones_like(scale)
        down_load.wait()

    row_stages(
        2, lambda k: None, TOKEN_MODES,
        t1_src, t1_dst, t2_src, t2_dst, t_whole, token_use, start_probes,
    )()

    def by_token(values, factor):
        return (values.reshape(probe_count, token_count, C) * factor[None]).reshape(M, C)

    def send_joined(k, value):
        blocks = value.reshape(N, R, C)
        joined[k] = blocks
        p1_src[k] = blocks.astype(BF16)

    def hidden_part(k):
        lhs = pushed[...].reshape(M, width)
        gate_tan = jnp.dot(lhs, gate_w[:, columns(k)], preferred_element_type=F32)
        up_tan = jnp.dot(lhs, up_w[:, columns(k)], preferred_element_type=F32)
        send_joined(k, by_token(gate_tan, slope[:, columns(k)]) + by_token(up_tan, act[:, columns(k)]))

    def add_to_acc(k, value):
        value = value.reshape(2, half, width)
        acc[...] = value if k == 0 else acc[...] + value

    def hidden_use(k):
        lhs = whole[k].reshape(M, C)
        add_to_acc(k, jnp.dot(lhs, down_w[columns(k), :], preferred_element_type=F32))

    def back_part(k):
        lhs = tangent[...].reshape(M, width)
        send_joined(k, lax.dot_general(lhs, down_w[columns(k), :], NT, preferred_element_type=F32))

    def back_use(k):
        piece = whole[k].reshape(M, C).astype(F32)
        gate_pull = by_token(piece, slope[:, columns(k)]).astype(BF16)
        up_pull = by_token(piece, act[:, columns(k)]).astype(BF16)
        value = lax.dot_general(gate_pull, gate_w[:, columns(k)], NT, preferred_element_type=F32)
        value += lax.dot_general(up_pull, up_w[:, columns(k)], NT, preferred_element_type=F32)
        add_to_acc(k, value)

    def col_half(phase, finish_row):
        swap = remote(acc.at[other], pair_in, pair_ss.at[0], pair_rs.at[0], partner)
        swap.start()
        total = acc[c]
        swap.wait_recv()
        total += pair_in[...]
        z_src[...] = total.astype(z_src.dtype)
        copies = [
            remote(z_src, z_dst.at[phase, d - 1], z_ss.at[0], z_rs.at[phase], z_peers[d])
            for d in range(1, NZ)
        ]
        for d in sorted(range(1, NZ), key=lambda d: -min(d, NZ - d)):
            copies[d - 1].start()
        acc[c] = total
        swap.wait_send()
        finish_row()
        wait_for(z_dst.at[phase], z_rs.at[phase])
        total = acc[c]
        for d in range(1, NZ):
            total += z_dst[phase, d - 1].astype(F32)
        wait_for(z_dst.at[phase], z_ss.at[0])
        return total

    def share(buffer, which):
        mine, theirs = buffer.at[c], buffer.at[other]
        send, recv = pair_ss.at[which], pair_rs.at[which]
        remote(mine, mine, send, recv, partner).start()
        remote(theirs, theirs, send, recv, partner).wait_recv()
        remote(mine, mine, send, recv, partner).wait_send()

    def folded(values):
        rows, lanes = values.shape
        total = None
        for r in range(0, rows, 8):
            for l in range(0, lanes, 128):
                piece = values[r : r + 8, l : l + 128]
                total = piece if total is None else total + piece
        return jnp.sum(total, axis=0, keepdims=True)

    def square_copies():
        return [
            remote(sq, sq_in.at[slot], sq_ss.at[0], sq_rs.at[0], row_peer(dx, dy))
            for slot, (dx, dy) in enumerate(row_offsets)
        ]

    def send_squares():
        for p in range(probe_count):
            i, j = divmod(p, half_probes)
            values = grown_all[i, j * token_count : (j + 1) * token_count]
            sq[p : p + 1] = folded(values * values)
        for cp in square_copies():
            cp.start()

    def levels():
        total = sq[...]
        wait_for(sq_in, sq_rs.at[0])
        for slot in range(len(row_offsets)):
            total += sq_in[slot]
        wait_for(sq_in, sq_ss.at[0])
        return jnp.sum(total, axis=1, keepdims=True) / entries

    def sweep(it, carry):
        def squares():
            @pl.when(it > 0)
            def _():
                send_squares()

        finish = row_stages(
            0, hidden_part, MODES,
            p1_src, p1_dst, p2_src, p2_dst.at[0], whole, hidden_use, squares,
        )
        total = col_half(0, finish)

        @pl.when(it > 0)
        def _():
            factor = lax.rsqrt(levels() + EPSILON)
            for p in range(probe_count):
                scale[p] = jnp.broadcast_to(factor[p : p + 1], scale.shape[1:])

        parts = [
            total[i * token_count : (i + 1) * token_count] * scale[c * half_probes + i, 0:1, 0:1]
            for i in range(half_probes)
        ]
        tangent[c] = jnp.concatenate(parts, axis=0).astype(BF16)
        share(tangent, 1)

        finish = row_stages(
            1, back_part, MODES,
            p1_src, p1_dst, p2_src, p2_dst.at[1], whole, back_use,
        )
        grown_all[c] = col_half(1, finish) * gain
        share(grown_all, 2)
        pushed[...] = (grown_all[...] * gain[None]).astype(BF16)
        return carry

    sq[...] = jnp.zeros_like(sq)
    lax.fori_loop(0, ITERS, sweep, 0)

    send_squares()
    out = pltpu.make_async_copy(grown_all, grown_hbm, small_sem.at[3])
    out.start()
    level_ref[...] = jnp.broadcast_to(levels(), level_ref.shape)
    out.wait()


def finish_kernel(grown_ref, level_ref, basis_ref, stretch_ref):
    probe_count = basis_ref.shape[0]
    level = level_ref[...]
    root = jnp.sqrt(level)
    factor = lax.rsqrt(level + EPSILON)
    lane = lax.broadcasted_iota(jnp.int32, (1, probe_count), 1)
    stretch = jnp.zeros((1, probe_count), F32)
    for p in range(probe_count):
        stretch = jnp.where(lane == p, root[p : p + 1, 0:1], stretch)
        basis_ref[p] = grown_ref[p] * factor[p : p + 1, 0:1]
    stretch_ref[...] = stretch


def solution(mesh, chunk=CHUNK, shape=(4, 4, 4, 2)):
    N, _, NZ, _ = shape
    torus = Mesh(mesh.devices.reshape(shape), ("x", "y", "z", "c"))
    row, col = ("x", "y"), ("z", "c")

    def local(tokens, gain, gate_weight, up_weight, down_weight, probes):
        probe_count, token_count, width = probes.shape
        hidden = gate_weight.shape[1]
        M = probe_count * token_count
        K, C = hidden // chunk, chunk
        R = M // N
        TR = 2 * token_count // N
        T1, T2, TG = TOKEN_TYPES
        entries = token_count * width * N * N
        cfg = (N, NZ, K, C, probe_count, token_count, entries)
        vm = pltpu.VMEM
        dma = pltpu.SemaphoreType.DMA
        grown, level = pl.pallas_call(
            functools.partial(kernel, cfg),
            out_shape=(
                jax.ShapeDtypeStruct((2, M // 2, width), F32),
                jax.ShapeDtypeStruct((8, 128), F32),
            ),
            in_specs=[pl.BlockSpec(memory_space=pl.ANY)] * 6,
            out_specs=(
                pl.BlockSpec(memory_space=pl.ANY),
                pl.BlockSpec(memory_space=pltpu.VMEM),
            ),
            scratch_shapes=[
                vm((token_count, width), BF16), vm((1, width), F32), vm(probes.shape, F32),
                vm((width, hidden), BF16), vm((width, hidden), BF16), vm((hidden, width), BF16),
                vm((token_count, hidden), F32), vm((token_count, hidden), F32),
                vm((2, M // 2, width), BF16), vm((2, M // 2, width), BF16), vm((2, M // 2, width), F32),
                vm((2, M // 2, width), F32),
                vm((K, N, R, C), F32), vm((K, N, R, C), BF16), vm((K, N - 1, R, C), BF16),
                vm((K, R, C), BF16), vm((2, K, N - 1, R, C), BF16), vm((K, N, R, C), BF16),
                vm((K, N, TR, C), F32), vm((K, N, TR, C), T1), vm((K, N - 1, TR, C), T1),
                vm((K, TR, C), T2), vm((K, N - 1, TR, C), T2), vm((K, N, TR, C), TG),
                vm((M // 2, width), F32), vm((M // 2, width), BF16), vm((2, NZ - 1, M // 2, width), BF16),
                vm((8, 128), F32), vm((N * N - 1, 8, 128), F32),
                vm((probe_count, 8, 128), F32),
                dma((4,)), dma((K,)), dma((K,)), dma((1,)),
                dma((1,)), dma((K,)), dma((1,)), dma((3, K)), dma((1,)), dma((K,)), dma((1,)), dma((K,)),
                dma((3,)), dma((3,)),
                dma((1,)), dma((2,)),
                dma((1,)), dma((1,)),
            ],
            compiler_params=pltpu.CompilerParams(collective_id=0, has_side_effects=True),
        )(tokens, gain.reshape(1, width), gate_weight, up_weight, down_weight, probes)
        basis, stretch = pl.pallas_call(
            finish_kernel,
            out_shape=(
                jax.ShapeDtypeStruct(probes.shape, F32),
                jax.ShapeDtypeStruct((1, probe_count), F32),
            ),
            in_specs=[pl.BlockSpec(memory_space=pltpu.VMEM)] * 2,
            out_specs=(
                pl.BlockSpec(memory_space=pltpu.VMEM),
                pl.BlockSpec(memory_space=pltpu.VMEM),
            ),
        )(grown.reshape(probes.shape), level)
        return basis, stretch.reshape(probe_count)

    return jax.shard_map(
        local,
        mesh=torus,
        in_specs=(P(None, row), P(row), P(row, col), P(row, col), P(col, row), P(None, None, row)),
        out_specs=(P(None, None, row), P()),
        check_vma=False,
    )
```

time: 193 us -> 189 us (0.979)
  local copies, waits for them, and re-layouts: 2.8 us -> 0 us
    unnamed x2 -> x0, local copies, waits for them, and re-layouts: 2.8 us -> none
    pallas_call x1, Pallas kernels: 189 us -> 186 us  [local(): pl.pallas_call(functools.partial(kernel, cfg), out_shape=(jax.ShapeDtypeS...]
where the time goes in v4:
time: 189 us
  Pallas kernels  188 us (99%)
    pallas_call x1, Pallas kernels, local(): pl.pallas_call(functools.partial(kernel, cfg), out_shape=(jax.ShapeDtypeS...  186 us

profile of v4, /device:TPU:1, one launch (start us, length us, event | category | flops | bytes accessed | tf_op | source)
XLA Modules:
  0.0 188.8 jit_solution(10930324530981647438)
XLA Ops:
  0.6 186.5 %shard_map.77 = (f32[2,64,512]{2,1,0:T(8,128)}, f32[8,128]{1,0:T(8,128)}) custom-call(bf16[32,512]{1,0:T(8,128)(2,1)} %tokens_hbm.1, f32[1,512]{1,0:T(1,128)} %bitcast.4, bf16[512,3584]{1,0:T(8,128)(2,1)} %gate_hbm.1, bf16[512,3584]{1,0:T(8,128)(2,1)} %up_hbm.1, bf16[3584,512]{1,0:T(8,128)(2,1)} %down_hbm.1, f32[4,32,512]{2,1,0:T(8,128)} %probes_hbm.1), custom_call_target="tpu_custom_call" | custom-call | tf_op jit(solution)/shard_map/pallas_call | solution.py:431
  187.1 1.7 shard_map.78

commit v5 on v4

--- a/solution.py
+++ b/solution.py
@@ -17,7 +17,7 @@
 CHUNK = 512
 MODES = (3, 3, 3, 3, 3, 3, 3)
 TOKEN_MODES = (3, 3, 3, 3, 3, 3, 3)
-TOKEN_TYPES = (BF16, F32, F32)
+TOKEN_TYPES = (BF16, BF16, F32)
 HOP = 3.0
 STEP = 0.5
 

time: 189 us -> 186 us (0.984)
  Pallas kernels: 188 us -> 186 us
    pallas_call x1, Pallas kernels: 186 us -> 184 us  [local(): pl.pallas_call(functools.partial(kernel, cfg), out_shape=(jax.ShapeDtypeS...]
where the time goes in v5:
time: 186 us
  Pallas kernels  186 us (100%)
    pallas_call x1, Pallas kernels, local(): pl.pallas_call(functools.partial(kernel, cfg), out_shape=(jax.ShapeDtypeS...  184 us

profile of v5, /device:TPU:1, one launch (start us, length us, event | category | flops | bytes accessed | tf_op | source)
XLA Modules:
  0.0 186.3 jit_solution(14772257722560826722)
XLA Ops:
  0.6 184.0 %shard_map.77 = (f32[2,64,512]{2,1,0:T(8,128)}, f32[8,128]{1,0:T(8,128)}) custom-call(bf16[32,512]{1,0:T(8,128)(2,1)} %tokens_hbm.1, f32[1,512]{1,0:T(1,128)} %bitcast.4, bf16[512,3584]{1,0:T(8,128)(2,1)} %gate_hbm.1, bf16[512,3584]{1,0:T(8,128)(2,1)} %up_hbm.1, bf16[3584,512]{1,0:T(8,128)(2,1)} %down_hbm.1, f32[4,32,512]{2,1,0:T(8,128)} %probes_hbm.1), custom_call_target="tpu_custom_call" | custom-call | tf_op jit(solution)/shard_map/pallas_call | solution.py:431
  184.6 1.7 shard_map.78

commit v6 on v5

--- a/solution.py
+++ b/solution.py
@@ -293,7 +293,7 @@
         value += lax.dot_general(up_pull, up_w[:, columns(k)], NT, preferred_element_type=F32)
         add_to_acc(k, value)
 
-    def col_half(phase, finish_row):
+    def col_half(phase, meanwhile):
         swap = remote(acc.at[other], pair_in, pair_ss.at[0], pair_rs.at[0], partner)
         swap.start()
         total = acc[c]
@@ -308,7 +308,7 @@
             copies[d - 1].start()
         acc[c] = total
         swap.wait_send()
-        finish_row()
+        meanwhile()
         wait_for(z_dst.at[phase], z_rs.at[phase])
         total = acc[c]
         for d in range(1, NZ):
@@ -364,14 +364,17 @@
             0, hidden_part, MODES,
             p1_src, p1_dst, p2_src, p2_dst.at[0], whole, hidden_use, squares,
         )
-        total = col_half(0, finish)
-
-        @pl.when(it > 0)
-        def _():
-            factor = lax.rsqrt(levels() + EPSILON)
-            for p in range(probe_count):
-                scale[p] = jnp.broadcast_to(factor[p : p + 1], scale.shape[1:])
-
+
+        def meanwhile():
+            finish()
+
+            @pl.when(it > 0)
+            def _():
+                factor = lax.rsqrt(levels() + EPSILON)
+                for p in range(probe_count):
+                    scale[p] = jnp.broadcast_to(factor[p : p + 1], scale.shape[1:])
+
+        total = col_half(0, meanwhile)
         parts = [
             total[i * token_count : (i + 1) * token_count] * scale[c * half_probes + i, 0:1, 0:1]
             for i in range(half_probes)

time: 186 us -> 186 us (level)
  no operation moved by 1% of the time
where the time goes in v6:
time: 186 us
  Pallas kernels  185 us (99%)
    pallas_call x1, Pallas kernels, local(): pl.pallas_call(functools.partial(kernel, cfg), out_shape=(jax.ShapeDtypeS...  184 us

profile of v6, /device:TPU:1, one launch (start us, length us, event | category | flops | bytes accessed | tf_op | source)
XLA Modules:
  0.0 186.1 jit_solution(4521359115266696728)
XLA Ops:
  0.6 183.7 %shard_map.77 = (f32[2,64,512]{2,1,0:T(8,128)}, f32[8,128]{1,0:T(8,128)}) custom-call(bf16[32,512]{1,0:T(8,128)(2,1)} %tokens_hbm.1, f32[1,512]{1,0:T(1,128)} %bitcast.4, bf16[512,3584]{1,0:T(8,128)(2,1)} %gate_hbm.1, bf16[512,3584]{1,0:T(8,128)(2,1)} %up_hbm.1, bf16[3584,512]{1,0:T(8,128)(2,1)} %down_hbm.1, f32[4,32,512]{2,1,0:T(8,128)} %probes_hbm.1), custom_call_target="tpu_custom_call" | custom-call | tf_op jit(solution)/shard_map/pallas_call | solution.py:434
  184.4 1.7 shard_map.78
